TPU v7x, 512 devices: a whole 4x4x16 slice. The times are simulated.
512 devices in a mesh: depth: 4 (over y_hi, core), blk: 128 (over z, x, y_lo).
Axes of the slice: x: 4, y: 4 (y_hi: 2, y_lo: 2; y = y_hi * 2 + y_lo), z: 16, core: 2. Of those that a mesh axis runs over, the one named last changes fastest.
Arguments:
- jacobian: bfloat16 [1536, 16384], P(('depth', 'blk')), may hold values from -6 to 6
- gain_inverse: bfloat16 [16384, 16384], P('depth', 'blk'), may hold values from -0.00024414062 to 0.00048828125, as said below
- variance: float32 [1536], P(('depth', 'blk')), may hold values from 2 to 12
Outputs:
- omega_diag: float32 [1536], P(('depth', 'blk'))
Inputs may be any that keep to these rules, and one draw needn't show every extreme that they name: gain_inverse is symmetric and positive definite.
All inputs are finite; a program needn't handle non-finite values.
Results may differ from a plain program's by a relative error of at most 0.0003.
Values may be sent and summed in bfloat16 or wider, within the bound.
No kernel may reach another device: no remote copies, remote signals or barrier semaphores. Data moves between devices by JAX's collectives and lax.ppermute only.
A program may use at most 128 MiB of HBM per device.

v0:
```python
import jax
import jax.numpy as jnp
from jax import lax
from jax.sharding import Mesh
from jax.sharding import PartitionSpec as P

BLK = ("blk_0", "blk_1", "blk_2")
DEPTH_BLK = ("depth", "blk_0", "blk_1", "blk_2")


def in_order(parts, dim):
    shape = list(parts.shape[1:])
    shape[dim] *= parts.shape[0]
    return jnp.moveaxis(parts, 0, dim).reshape(shape)


def copy_for_each(shard, axis):
    copies = jnp.broadcast_to(shard, (lax.axis_size(axis), *shard.shape))
    return lax.all_to_all(copies, axis, split_axis=0, concat_axis=0, tiled=True)


def collect(shard, axis, dim):
    return in_order(copy_for_each(shard, axis), dim)


def edges_of(length, count):
    unit = 8 if length >= 8 * count else 1
    return [length // unit * k // count * unit for k in range(1, count)]


def gather_in_order(shard, axes, turns):
    parts = shard[None]
    for k in turns:
        parts = lax.all_gather(parts, axes[k], axis=0, tiled=True)
    current = [lax.axis_size(axes[k]) for k in reversed(turns)]
    parts = parts.reshape(*current, *shard.shape)
    turned = sorted(range(len(turns)), key=lambda place: turns[len(turns) - 1 - place])
    return parts.transpose(*turned, *range(len(turns), parts.ndim)).reshape(-1, *shard.shape)


def gather_all_axes(shard, axes, dim):
    numbers = list(range(len(axes)))[::-1]
    cut = shard.shape.index(max(shard.shape[:-1] or shard.shape))
    edges = [0, *edges_of(shard.shape[cut], len(axes)), shard.shape[cut]]
    gathered = []
    for k, (start, end) in enumerate(zip(edges, edges[1:])):
        if end > start:
            slab = lax.slice_in_dim(shard, start, end, axis=cut)
            gathered.append(gather_in_order(slab, axes, numbers[k:] + numbers[:k]))
    return in_order(jnp.concatenate(gathered, axis=cut + 1), dim)


def shards(jacobian, gain_inverse, variance):
    rows_local = jacobian.shape[0]
    width = jacobian.shape[1]
    depth_count = lax.axis_size("depth")
    blk_count = lax.axis_size(BLK)
    panel_width = width // blk_count
    quarter_rows = lax.all_to_all(jacobian, "depth", split_axis=1, concat_axis=0, tiled=True)
    by_blk = lax.all_to_all(jacobian, BLK, split_axis=1, concat_axis=0, tiled=True)
    flat = by_blk.reshape(blk_count, rows_local * panel_width)
    joined = collect(flat, "depth", 1)
    panel = joined.reshape(blk_count * depth_count * rows_local, panel_width)
    gathered = gather_all_axes(quarter_rows, BLK, 0)
    projected = jnp.dot(gathered, gain_inverse, preferred_element_type=jnp.float32)
    partials = jnp.sum(projected * panel.astype(jnp.float32), axis=1)
    ordered = partials.reshape(blk_count, depth_count, rows_local).transpose(1, 0, 2).reshape(-1)
    quadratic = lax.psum_scatter(ordered, DEPTH_BLK, scatter_dimension=0, tiled=True)
    return variance - quadratic


def solution(mesh):
    split = Mesh(
        mesh.devices.reshape(mesh.shape["depth"], 16, 4, 2), ("depth", "blk_0", "blk_1", "blk_2")
    )
    return jax.shard_map(
        shards,
        mesh=split,
        in_specs=(P(DEPTH_BLK, None), P("depth", BLK), P(DEPTH_BLK)),
        out_specs=P(DEPTH_BLK),
        check_vma=False,
    )
```

profile of v0, /device:TPU:1, one launch (start us, length us, event | category | flops | bytes accessed | tf_op | source)
XLA Modules:
  0.0 513.9 jit_solution(17710025762078432333)
XLA Ops:
  6.5 0.0 copy-start
  6.5 0.0 all-gather.18.cloned.1.call-start
  6.5 15.3 %all_to_all.40 = bf16[3,4,4096]{2,0,1:T(4,128)(2,1)S(1)} all-to-all(bf16[3,4,4096]{2,0,1:T(4,128)(2,1)} %bitcast.30), channel_id=1, replica_groups=mesh['depth'=4,'blk_0'=16,'blk_1'=4,'blk_2'=2] {'depth'}, dimensions={1} | all-to-all | bytes 196608 | tf_op jit(solution)/shard_map/all_to_all | solution.py:59
  21.9 0.1 all_to_all.32
  22.0 29.5 %all-gather.5 = bf16[16,4,4096]{2,1,0:T(4,128)(2,1)} all-gather(bf16[1,4,4096]{2,1,0:T(4,128)(2,1)S(1)} %get-tuple-element.6), channel_id=4, replica_groups=mesh['depth'=4,'blk_0'=16,'blk_1'=4,'blk_2'=2] {'blk_0'}, dimensions={0}, use_global_device_ids=true | all-gather | bytes 557056 | tf_op jit(solution)/shard_map/all_gather | solution.py:34
  51.5 0.0 all-gather.18.cloned.1.call-update
  51.6 0.0 all-gather.14.cloned.1.call-start
  51.6 10.2 %all-gather.4 = bf16[4,4,4096]{2,1,0:T(4,128)(2,1)} all-gather(bf16[1,4,4096]{2,1,0:T(4,128)(2,1)S(1)} %get-tuple-element.7), channel_id=3, replica_groups=mesh['depth'=4,'blk_0'=16,'blk_1'=4,'blk_2'=2] {'blk_1'}, dimensions={0}, use_global_device_ids=true | all-gather | bytes 163840 | tf_op jit(solution)/shard_map/all_gather | solution.py:34
  61.8 0.0 all-gather.14.cloned.1.call-update
  61.8 0.0 all-gather.20.cloned.1.call-start
  61.9 21.9 %all-gather.18.cloned.1.call-done = bf16[32,4,4096]{2,1,0:T(4,128)(2,1)} async-done(((bf16[16,4,4096]{2,1,0:T(4,128)(2,1)}), bf16[32,4,4096]{2,1,0:T(4,128)(2,1)}) %all-gather.18.cloned.1.call-update) | async-done | bytes 1048592 | tf_op jit(solution)/shard_map/all_gather | solution.py:34
  83.7 0.0 all-gather.20.cloned.1.call-update
  83.8 0.0 all-gather.16.cloned.1.call-start
  83.8 66.7 %all-gather.14.cloned.1.call-done = bf16[64,4,4096]{2,1,0:T(4,128)(2,1)} async-done(((bf16[4,4,4096]{2,1,0:T(4,128)(2,1)}), bf16[64,4,4096]{2,1,0:T(4,128)(2,1)}) %all-gather.14.cloned.1.call-update) | async-done | bytes 2097168 | tf_op jit(solution)/shard_map/all_gather | solution.py:34
  150.5 0.0 all-gather.16.cloned.1.call-update
  150.5 0.0 all-gather.12.cloned.1.call-start
  150.6 3.7 all-gather.3
  154.2 10.6 %all_gather.28 = bf16[8,4,4096]{2,1,0:T(4,128)(2,1)} all-gather(bf16[2,4,4096]{2,1,0:T(4,128)(2,1)S(1)} %all-gather.3), channel_id=1, replica_groups=mesh['depth'=4,'blk_0'=16,'blk_1'=4,'blk_2'=2] {'blk_1'}, dimensions={0}, use_global_device_ids=true | all-gather | bytes 327680 | tf_op jit(solution)/shard_map/all_gather | solution.py:34
  164.8 0.0 all-gather.12.cloned.1.call-update
  164.8 26.2 %all_to_all.41 = bf16[3,128,128]{2,0,1:T(4,128)(2,1)S(1)} all-to-all(bf16[3,128,128]{2,0,1:T(4,128)(2,1)} %bitcast.31), channel_id=1, replica_groups=mesh['depth'=4,'blk_0'=16,'blk_1'=4,'blk_2'=2] {'blk_0','blk_1','blk_2'}, dimensions={1} | all-to-all | bytes 196608 | tf_op jit(solution)/shard_map/all_to_all | solution.py:60
  191.0 0.1 copy.23
  191.1 0.1 copy.24
  191.3 0.8 broadcast_in_dim.15
  192.1 19.0 %all-to-all-start.2 = ((bf16[4,128,384]{2,1,0:T(8,128)(2,1)}), bf16[4,128,384]{2,1,0:T(8,128)(2,1)S(1)}, u32[]{:S(2)}, u32[]{:S(2)}) async-start(bf16[4,128,384]{2,1,0:T(8,128)(2,1)} %broadcast_in_dim.15), calls=%async_computation.2 | async-start | bytes 786432 | tf_op jit(solution)/shard_map/all_to_all | solution.py:19
  211.0 7.9 %all-to-all-done.2 = bf16[4,128,384]{2,1,0:T(8,128)(2,1)S(1)} async-done(((bf16[4,128,384]{2,1,0:T(8,128)(2,1)}), bf16[4,128,384]{2,1,0:T(8,128)(2,1)S(1)}, u32[]{:S(2)}, u32[]{:S(2)}) %all-to-all-start.2) | async-done | bytes 393248 | tf_op jit(solution)/shard_map/all_to_all | solution.py:19
  219.0 0.1 convert_bitcast_fusion
  219.0 0.5 copy.25
  219.5 0.3 reshape.41
  219.9 0.3 copy.26
  220.1 0.0 all-gather.20.cloned.1.call-done
  220.2 7.9 %copy.21 = bf16[4,2,16,4,4096]{4,3,1,0,2:T(4,128)(2,1)} copy(bf16[4,2,16,4,4096]{4,3,2,1,0:T(4,128)(2,1)} %bitcast.27) | data formatting | bytes 8388608 | tf_op jit(solution)/shard_map/reshape | solution.py:36
  228.0 56.5 %all-gather.16.cloned.1.call-done = bf16[128,4,4096]{2,1,0:T(4,128)(2,1)} async-done(((bf16[64,4,4096]{2,1,0:T(4,128)(2,1)}), bf16[128,4,4096]{2,1,0:T(4,128)(2,1)}) %all-gather.16.cloned.1.call-update) | async-done | bytes 4194320 | tf_op jit(solution)/shard_map/all_gather | solution.py:34
  284.5 7.9 %copy.20 = bf16[2,16,4,4,4096]{4,3,0,2,1:T(4,128)(2,1)} copy(bf16[2,16,4,4,4096]{4,3,2,1,0:T(4,128)(2,1)} %bitcast.28) | data formatting | bytes 8388608 | tf_op jit(solution)/shard_map/reshape | solution.py:36
  292.4 64.5 %all-gather.12.cloned.1.call-done = bf16[128,4,4096]{2,1,0:T(4,128)(2,1)} async-done(((bf16[8,4,4096]{2,1,0:T(4,128)(2,1)}), bf16[128,4,4096]{2,1,0:T(4,128)(2,1)}) %all-gather.12.cloned.1.call-update) | async-done | bytes 4194320 | tf_op jit(solution)/shard_map/all_gather | solution.py:34
  356.9 12.1 %pad_maximum_fusion = bf16[128,12,4096]{2,1,0:T(8,128)(2,1)} fusion(bf16[128,4,4096]{2,1,0:T(4,128)(2,1)} %bitcast.25, bf16[128,4,4096]{2,1,0:T(4,128)(2,1)} %bitcast.26, bf16[128,4,4096]{2,1,0:T(4,128)(2,1)} %all-gather.12.cloned.1.call-done), kind=kLoop, calls=%fused_computation | loop fusion | flops 37748736 | bytes 25165824 | tf_op jit(solution)/shard_map/concatenate | solution.py:50
  369.0 18.1 %reshape.37 = bf16[1536,4096]{1,0:T(8,128)(2,1)} reshape(bf16[128,12,4096]{2,1,0:T(8,128)(2,1)} %pad_maximum_fusion) | data formatting | bytes 25165824 | tf_op jit(solution)/shard_map/reshape | solution.py:14
  387.1 0.0 copy-done
  387.1 0.0 copy-start.1
  387.1 8.9 %fusion = f32[1536]{0:T(1024)S(1)} fusion(f32[1536,128]{0,1:T(8,128)S(1)} %copy.26, bf16[1536,4096]{1,0:T(8,128)(2,1)} %reshape.37, bf16[4096,128]{1,0:T(8,128)(2,1)S(1)} %copy-done), kind=kOutput, calls=%fused_computation.2 | convolution fusion | flops 1611004416 | bytes 14424064 | tf_op jit(solution)/shard_map/dot_general | solution.py:65
  396.1 0.3 reshape.39
  396.4 0.2 reshape.40
  396.6 110.2 %all-reduce = f32[1536]{0:T(1024)S(1)} all-reduce(f32[1536]{0:T(1024)S(1)} %reshape.40), channel_id=5, replica_groups=mesh['depth'=4,'blk_0'=16,'blk_1'=4,'blk_2'=2] {'depth','blk_0','blk_1',..., use_global_device_ids=true, to_apply=%region_1.0.clone | all-reduce | flops 1536 | bytes 12288
  506.8 0.0 copy-done.1
  506.8 0.6 dynamic-slice_subtract_fusion
  (2 shorter events, 0.1 us)
Async XLA Ops:
  6.5 380.6 %copy-start = (bf16[4096,128]{1,0:T(8,128)(2,1)S(1)}, bf16[4096,128]{1,0:T(8,128)(2,1)}, u32[]{:S(2)}) copy-start(bf16[4096,128]{1,0:T(8,128)(2,1)} %param.4) | copy-start | bytes 3145732
  6.5 77.2 %all-gather.18.cloned.1.call-start = ((), (), s32[]{:S(2)}) async-start(), calls=%async_computation.6 | async-start | bytes 1572864 | tf_op jit(solution)/shard_map/all_gather | solution.py:34
  51.6 98.9 %all-gather.14.cloned.1.call-start = ((), (), s32[]{:S(2)}) async-start(), calls=%async_computation.4 | async-start | bytes 2228224 | tf_op jit(solution)/shard_map/all_gather | solution.py:34
  61.8 158.3 %all-gather.20.cloned.1.call-start = ((), (), s32[]{:S(2)}) async-start(), calls=%async_computation.7 | async-start | bytes 5242880 | tf_op jit(solution)/shard_map/all_gather | solution.py:34
  83.8 200.7 %all-gather.16.cloned.1.call-start = ((), (), s32[]{:S(2)}) async-start(), calls=%async_computation.5 | async-start | bytes 6291456 | tf_op jit(solution)/shard_map/all_gather | solution.py:34
  150.5 206.4 %all-gather.12.cloned.1.call-start = ((), (), s32[]{:S(2)}) async-start(), calls=%async_computation.3 | async-start | bytes 4456448 | tf_op jit(solution)/shard_map/all_gather | solution.py:34
  192.1 26.9 %all-to-all-start.2 = ((bf16[4,128,384]{2,1,0:T(8,128)(2,1)}), bf16[4,128,384]{2,1,0:T(8,128)(2,1)S(1)}, u32[]{:S(2)}, u32[]{:S(2)}) async-start(bf16[4,128,384]{2,1,0:T(8,128)(2,1)} %broadcast_in_dim.15), calls=%async_computation.2 | async-start | bytes 786432 | tf_op jit(solution)/shard_map/all_to_all | solution.py:19
  387.1 119.6 %copy-start.1 = (f32[3]{0:T(128)S(1)}, f32[3]{0:T(128)}, u32[]{:S(2)}) copy-start(f32[3]{0:T(128)} %param.5) | copy-start | bytes 40
Sparse Core Ops, SparseCore 0:
  51.7 32.0 all-gather.17
  85.8 64.6 all-gather.13
  152.6 63.1 all-gather.19
  217.7 66.7 all-gather.15
  286.4 70.4 all-gather.11
where the time goes:
time: 515 us; the launch traced here: 514 us
  waiting for transfers between devices  218 us (42%)
  blocking collectives  206 us (40%)
  local copies, waits for them, and re-layouts  36.6 us (7%)
  starting transfers between devices  19.1 us (4%)
  between operations  13.2 us (3%)
  other arithmetic  12.8 us (2%)
  matrix products  8.9 us (2%)
    all_gather x5, waiting for transfers between devices, gather_in_order(): parts = lax.all_gather(parts, axes[k], axis=0, tiled=True)  210 us
    unnamed x1, blocking collectives  110 us
    all_gather x4, blocking collectives, gather_in_order(): parts = lax.all_gather(parts, axes[k], axis=0, tiled=True)  54 us
    all_to_all x1, blocking collectives, shards(): lax.all_to_all(jacobian, BLK, split_axis=1, concat_axis=0, tiled=True)  26.2 us
    all_to_all x1, starting transfers between devices, copy_for_each(): return lax.all_to_all(copies, axis, split_axis=0, concat_axis=0, tiled=True)  19 us
    reshape x1, local copies, waits for them, and re-layouts, in_order(): return jnp.moveaxis(parts, 0, dim).reshape(shape)  18.1 us
    reshape x2, local copies, waits for them, and re-layouts, gather_in_order(): parts = parts.reshape(*current, *shard.shape)  15.7 us
    all_to_all x1, blocking collectives, shards(): lax.all_to_all(jacobian, 'depth', split_axis=1, concat_axis=0, tiled=True)  15.3 us
  transfers between devices with their start and end apart: 6, of which 5 were waited for; matrix products, arithmetic and copies ran while one was open for 3% of the time, Pallas kernels for 0%

commit v1 on v0

--- a/solution.py
+++ b/solution.py
@@ -6,6 +6,11 @@
 
 BLK = ("blk_0", "blk_1", "blk_2")
 DEPTH_BLK = ("depth", "blk_0", "blk_1", "blk_2")
+
+
+def exchange_gather(block, axis, dim):
+    stack = jnp.stack([block] * lax.axis_size(axis))
+    return jnp.concatenate(lax.all_to_all(stack, axis, 0, 0), axis=dim)
 
 
 def in_order(parts, dim):
@@ -31,7 +36,7 @@
 def gather_in_order(shard, axes, turns):
     parts = shard[None]
     for k in turns:
-        parts = lax.all_gather(parts, axes[k], axis=0, tiled=True)
+        parts = exchange_gather(parts, axes[k], 0)
     current = [lax.axis_size(axes[k]) for k in reversed(turns)]
     parts = parts.reshape(*current, *shard.shape)
     turned = sorted(range(len(turns)), key=lambda place: turns[len(turns) - 1 - place])

time: 515 us -> 681 us (1.32)
  waiting for transfers between devices: 218 us -> 326 us
  starting transfers between devices: 19.1 us -> 47.9 us
  blocking collectives: 206 us -> 233 us
  between operations: 13.2 us -> 0.17 us
  local copies, waits for them, and re-layouts: 36.6 us -> 46.6 us
    all_to_all x0 -> x4, waiting for transfers between devices: none -> 319 us  [exchange_gather(): return jnp.concatenate(lax.all_to_all(stack, axis, 0, 0), axis=dim)]
    all_gather x5 -> x0, waiting for transfers between devices: 210 us -> none  [gather_in_order(): parts = lax.all_gather(parts, axes[k], axis=0, tiled=True)]
    all_to_all x0 -> x5, blocking collectives: none -> 86.2 us  [exchange_gather(): return jnp.concatenate(lax.all_to_all(stack, axis, 0, 0), axis=dim)]
    all_gather x4 -> x0, blocking collectives: 54 us -> none  [gather_in_order(): parts = lax.all_gather(parts, axes[k], axis=0, tiled=True)]
    all_to_all x0 -> x4, starting transfers between devices: none -> 35.8 us  [exchange_gather(): return jnp.concatenate(lax.all_to_all(stack, axis, 0, 0), axis=dim)]
    another operation x0 -> x9, local copies, waits for them, and re-layouts: none -> 15.8 us  [the longest x8 11.9 us: exchange_gather(): stack = jnp.stack([block] * lax.axis_size(axis))]
    reshape x2 -> x0, local copies, waits for them, and re-layouts: 15.7 us -> none  [gather_in_order(): parts = parts.reshape(*current, *shard.shape)]
    unnamed x1, blocking collectives: 110 us -> 102 us
  transfers between devices with their start and end apart: 6 -> 5, of which waited for: 5 -> 5; matrix products, arithmetic and copies ran while one was open for 3% -> 3% of each run, Pallas kernels for 0% -> 0%
where the time goes in v1:
time: 681 us; the launch traced here: 679 us
  waiting for transfers between devices  326 us (48%)
  blocking collectives  233 us (34%)
  starting transfers between devices  47.9 us (7%)
  local copies, waits for them, and re-layouts  46.6 us (7%)
  other arithmetic  17.1 us (3%)
  matrix products  8.9 us (1%)
    all_to_all x4, waiting for transfers between devices, exchange_gather(): return jnp.concatenate(lax.all_to_all(stack, axis, 0, 0), axis=dim)  319 us
    unnamed x1, blocking collectives  102 us
    all_to_all x5, blocking collectives, exchange_gather(): return jnp.concatenate(lax.all_to_all(stack, axis, 0, 0), axis=dim)  86.2 us
    all_to_all x4, starting transfers between devices, exchange_gather(): return jnp.concatenate(lax.all_to_all(stack, axis, 0, 0), axis=dim)  35.8 us
    all_to_all x1, blocking collectives, shards(): lax.all_to_all(jacobian, BLK, split_axis=1, concat_axis=0, tiled=True)  28.7 us
    reshape x1, local copies, waits for them, and re-layouts, in_order(): return jnp.moveaxis(parts, 0, dim).reshape(shape)  18.1 us
    all_to_all x1, blocking collectives, shards(): lax.all_to_all(jacobian, 'depth', split_axis=1, concat_axis=0, tiled=True)  15.3 us
  transfers between devices with their start and end apart: 5, of which 5 were waited for; matrix products, arithmetic and copies ran while one was open for 3% of the time, Pallas kernels for 0%

profile of v1, /device:TPU:1, one launch (start us, length us, event | category | flops | bytes accessed | tf_op | source)
XLA Modules:
  0.0 679.4 jit_solution(11067693507656661145)
XLA Ops:
  0.0 0.0 copy-start
  0.0 15.3 %all_to_all.85 = bf16[3,4,4096]{2,0,1:T(4,128)(2,1)S(1)} all-to-all(bf16[3,4,4096]{2,0,1:T(4,128)(2,1)} %bitcast.37), channel_id=1, replica_groups=mesh['depth'=4,'blk_0'=16,'blk_1'=4,'blk_2'=2] {'depth'}, dimensions={1} | all-to-all | bytes 196608 | tf_op jit(solution)/shard_map/all_to_all | solution.py:64
  15.3 0.1 all_to_all.59
  15.5 5.3 all_to_all.86
  20.9 7.2 %all_to_all.87 = bf16[4,1,4,4096]{3,2,1,0:T(4,128)(2,1)S(1)} all-to-all(bf16[4,1,4,4096]{3,2,1,0:T(4,128)(2,1)S(1)} %stack.30), channel_id=1, replica_groups=mesh['depth'=4,'blk_0'=16,'blk_1'=4,'blk_2'=2] {'blk_1'}, dimensions={0} | all-to-all | bytes 262144 | tf_op jit(solution)/shard_map/all_to_all | solution.py:13
  28.1 0.1 stack.28
  28.2 8.6 %all_to_all.88 = bf16[4,2,4,4096]{3,2,1,0:T(4,128)(2,1)} all-to-all(bf16[4,2,4,4096]{3,2,1,0:T(4,128)(2,1)S(1)} %stack.28), channel_id=1, replica_groups=mesh['depth'=4,'blk_0'=16,'blk_1'=4,'blk_2'=2] {'blk_1'}, dimensions={0} | all-to-all | bytes 524288 | tf_op jit(solution)/shard_map/all_to_all | solution.py:13
  36.8 28.7 %all_to_all.89 = bf16[3,128,128]{2,0,1:T(4,128)(2,1)S(1)} all-to-all(bf16[3,128,128]{2,0,1:T(4,128)(2,1)} %bitcast.38), channel_id=1, replica_groups=mesh['depth'=4,'blk_0'=16,'blk_1'=4,'blk_2'=2] {'blk_0','blk_1','blk_2'}, dimensions={1} | all-to-all | bytes 196608 | tf_op jit(solution)/shard_map/all_to_all | solution.py:65
  65.4 1.0 stack.33
  66.4 4.2 all-to-all-start.7
  70.6 0.1 copy.30
  70.8 0.1 copy.31
  70.9 20.3 %all-to-all-done.7 = bf16[16,1,4,4096]{3,2,1,0:T(4,128)(2,1)S(1)} async-done(((bf16[16,1,4,4096]{3,2,1,0:T(4,128)(2,1)}), bf16[16,1,4,4096]{3,2,1,0:T(4,128)(2,1)S(1)}, u32[]{:S(2)}, u32[]{:S(2)}) %all-to-all-start.7) | async-done | bytes 524320 | tf_op jit(solution)/shard_map/all_to_all | solution.py:13
  91.2 0.8 broadcast_in_dim.3
  92.0 12.1 %all-to-all-start.11 = ((bf16[4,128,384]{2,1,0:T(8,128)(2,1)}), bf16[4,128,384]{2,1,0:T(8,128)(2,1)S(1)}, u32[]{:S(2)}, u32[]{:S(2)}) async-start(bf16[4,128,384]{2,1,0:T(8,128)(2,1)} %broadcast_in_dim.3), calls=%async_computation.11 | async-start | bytes 786432 | tf_op jit(solution)/shard_map/all_to_all | solution.py:24
  104.0 0.5 pad_maximum_fusion.2
  104.5 0.6 copy.26
  105.1 6.9 %all-to-all-done.11 = bf16[4,128,384]{2,1,0:T(8,128)(2,1)S(1)} async-done(((bf16[4,128,384]{2,1,0:T(8,128)(2,1)}), bf16[4,128,384]{2,1,0:T(8,128)(2,1)S(1)}, u32[]{:S(2)}, u32[]{:S(2)}) %all-to-all-start.11) | async-done | bytes 393248 | tf_op jit(solution)/shard_map/all_to_all | solution.py:24
  112.0 15.9 %all_to_all.90 = bf16[2,16,4,4096]{3,1,2,0:T(8,128)(2,1)} all-to-all(bf16[2,16,4,4096]{3,1,2,0:T(8,128)(2,1)S(1)} %copy.26), channel_id=1, replica_groups=mesh['depth'=4,'blk_0'=16,'blk_1'=4,'blk_2'=2] {'blk_2'}, dimensions={0} | all-to-all | bytes 2097152 | tf_op jit(solution)/shard_map/all_to_all | solution.py:13
  127.9 2.4 stack.31
  130.3 6.8 %all-to-all-start.5 = ((bf16[16,4,4,4096]{3,2,1,0:T(4,128)(2,1)}), bf16[16,4,4,4096]{3,2,1,0:T(4,128)(2,1)S(1)}, u32[]{:S(2)}, u32[]{:S(2)}) async-start(bf16[16,4,4,4096]{3,2,1,0:T(4,128)(2,1)} %stack.31), calls=%async_computation.5 | async-start | bytes 4194304 | tf_op jit(solution)/shard_map/all_to_all | solution.py:13
  137.1 2.3 copy.27
  139.4 89.6 %all-to-all-done.5 = bf16[16,4,4,4096]{3,2,1,0:T(4,128)(2,1)S(1)} async-done(((bf16[16,4,4,4096]{3,2,1,0:T(4,128)(2,1)}), bf16[16,4,4,4096]{3,2,1,0:T(4,128)(2,1)S(1)}, u32[]{:S(2)}, u32[]{:S(2)}) %all-to-all-start.5) | async-done | bytes 2097184 | tf_op jit(solution)/shard_map/all_to_all | solution.py:13
  229.0 3.7 stack.35
  232.7 4.8 all-to-all-start.9
  237.6 3.9 pad_maximum_fusion.1
  241.4 40.2 %all-to-all-done.9 = bf16[4,32,4,4096]{3,1,2,0:T(8,128)(2,1)} async-done(((bf16[4,32,4,4096]{3,1,2,0:T(8,128)(2,1)}), bf16[4,32,4,4096]{3,1,2,0:T(8,128)(2,1)}, u32[]{:S(2)}, u32[]{:S(2)}) %all-to-all-start.9) | async-done | bytes 4194336 | tf_op jit(solution)/shard_map/all_to_all | solution.py:13
  281.6 49.1 %all_to_all.91 = bf16[2,64,4,4096]{3,2,1,0:T(4,128)(2,1)} all-to-all(bf16[2,64,4,4096]{3,2,1,0:T(4,128)(2,1)} %pad_maximum_fusion.1), channel_id=1, replica_groups=mesh['depth'=4,'blk_0'=16,'blk_1'=4,'blk_2'=2] {'blk_2'}, dimensions={0} | all-to-all | bytes 8388608 | tf_op jit(solution)/shard_map/all_to_all | solution.py:13
  330.7 0.0 copy-done.2
  330.7 4.1 stack.29
  334.7 20.0 %all-to-all-start.3 = ((bf16[16,8,4,4096]{3,2,1,0:T(4,128)(2,1)}), bf16[16,8,4,4096]{3,2,1,0:T(4,128)(2,1)}, u32[]{:S(2)}, u32[]{:S(2)}) async-start(bf16[16,8,4,4096]{3,2,1,0:T(4,128)(2,1)} %stack.29), calls=%async_computation.3 | async-start | bytes 8388608 | tf_op jit(solution)/shard_map/all_to_all | solution.py:13
  354.8 0.1 convert_bitcast_fusion
  354.8 0.5 copy.32
  355.3 0.3 reshape.45
  355.7 0.3 copy.33
  355.9 0.0 copy-start.1
  355.9 7.5 %copy.28 = bf16[16,4,2,4,4096]{4,3,2,1,0:T(4,128)(2,1)} copy(bf16[16,4,2,4,4096]{4,0,2,3,1:T(8,128)(2,1)} %bitcast.14) | data formatting | bytes 8388608 | tf_op jit(solution)/shard_map/transpose | solution.py:43
  363.5 0.0 copy-done.1
  363.5 4.0 copy.25
  367.5 169.1 %all-to-all-done.3 = bf16[16,8,4,4096]{3,2,1,0:T(4,128)(2,1)} async-done(((bf16[16,8,4,4096]{3,2,1,0:T(4,128)(2,1)}), bf16[16,8,4,4096]{3,2,1,0:T(4,128)(2,1)}, u32[]{:S(2)}, u32[]{:S(2)}) %all-to-all-start.3) | async-done | bytes 4194336 | tf_op jit(solution)/shard_map/all_to_all | solution.py:13
  536.6 12.1 %pad_maximum_fusion = bf16[128,12,4096]{2,1,0:T(8,128)(2,1)} fusion(bf16[128,4,4096]{2,1,0:T(4,128)(2,1)} %bitcast.28, bf16[128,4,4096]{2,1,0:T(4,128)(2,1)} %bitcast.29, bf16[128,4,4096]{2,1,0:T(4,128)(2,1)} %bitcast.5), kind=kLoop, calls=%fused_computation | loop fusion | flops 37748736 | bytes 25165824 | tf_op jit(solution)/shard_map/concatenate | solution.py:55
  548.7 18.1 %reshape.41 = bf16[1536,4096]{1,0:T(8,128)(2,1)} reshape(bf16[128,12,4096]{2,1,0:T(8,128)(2,1)} %pad_maximum_fusion) | data formatting | bytes 25165824 | tf_op jit(solution)/shard_map/reshape | solution.py:19
  566.9 0.0 copy-done
  566.9 8.9 %fusion = f32[1536]{0:T(1024)S(1)} fusion(f32[1536,128]{0,1:T(8,128)S(1)} %copy.33, bf16[1536,4096]{1,0:T(8,128)(2,1)} %reshape.41, bf16[4096,128]{1,0:T(8,128)(2,1)S(1)} %copy-done), kind=kOutput, calls=%fused_computation.3 | convolution fusion | flops 1611004416 | bytes 14424064 | tf_op jit(solution)/shard_map/dot_general | solution.py:70
  575.8 0.3 reshape.43
  576.1 0.2 reshape.44
  576.3 102.5 %all-reduce = f32[1536]{0:T(1024)S(1)} all-reduce(f32[1536]{0:T(1024)S(1)} %reshape.44), channel_id=2, replica_groups=mesh['depth'=4,'blk_0'=16,'blk_1'=4,'blk_2'=2] {'depth','blk_0','blk_1',..., use_global_device_ids=true, to_apply=%region_1.0.clone | all-reduce | flops 1536 | bytes 12288
  678.8 0.6 dynamic-slice_subtract_fusion
  (7 shorter events, 0.1 us)
Async XLA Ops:
  0.0 566.9 %copy-start = (bf16[4096,128]{1,0:T(8,128)(2,1)S(1)}, bf16[4096,128]{1,0:T(8,128)(2,1)}, u32[]{:S(2)}) copy-start(bf16[4096,128]{1,0:T(8,128)(2,1)} %param.4) | copy-start | bytes 3145732
  66.4 24.8 %all-to-all-start.7 = ((bf16[16,1,4,4096]{3,2,1,0:T(4,128)(2,1)}), bf16[16,1,4,4096]{3,2,1,0:T(4,128)(2,1)S(1)}, u32[]{:S(2)}, u32[]{:S(2)}) async-start(bf16[16,1,4,4096]{3,2,1,0:T(4,128)(2,1)} %stack.33), calls=%async_computation.7 | async-start | bytes 1048576 | tf_op jit(solution)/shard_map/all_to_all | solution.py:13
  92.0 20.0 %all-to-all-start.11 = ((bf16[4,128,384]{2,1,0:T(8,128)(2,1)}), bf16[4,128,384]{2,1,0:T(8,128)(2,1)S(1)}, u32[]{:S(2)}, u32[]{:S(2)}) async-start(bf16[4,128,384]{2,1,0:T(8,128)(2,1)} %broadcast_in_dim.3), calls=%async_computation.11 | async-start | bytes 786432 | tf_op jit(solution)/shard_map/all_to_all | solution.py:24
  130.3 98.7 %all-to-all-start.5 = ((bf16[16,4,4,4096]{3,2,1,0:T(4,128)(2,1)}), bf16[16,4,4,4096]{3,2,1,0:T(4,128)(2,1)S(1)}, u32[]{:S(2)}, u32[]{:S(2)}) async-start(bf16[16,4,4,4096]{3,2,1,0:T(4,128)(2,1)} %stack.31), calls=%async_computation.5 | async-start | bytes 4194304 | tf_op jit(solution)/shard_map/all_to_all | solution.py:13
  232.7 48.9 %all-to-all-start.9 = ((bf16[4,32,4,4096]{3,1,2,0:T(8,128)(2,1)}), bf16[4,32,4,4096]{3,1,2,0:T(8,128)(2,1)}, u32[]{:S(2)}, u32[]{:S(2)}) async-start(bf16[4,32,4,4096]{3,1,2,0:T(8,128)(2,1)} %stack.35), calls=%async_computation.9 | async-start | bytes 8388608 | tf_op jit(solution)/shard_map/all_to_all | solution.py:13
  241.4 89.3 %copy-start.2 = (bf16[4,2,4,4096]{3,2,1,0:T(4,128)(2,1)S(1)}, bf16[4,2,4,4096]{3,2,1,0:T(4,128)(2,1)}, u32[]{:S(2)}) copy-start(bf16[4,2,4,4096]{3,2,1,0:T(4,128)(2,1)} %all_to_all.88) | copy-start | bytes 786436
  334.7 201.9 %all-to-all-start.3 = ((bf16[16,8,4,4096]{3,2,1,0:T(4,128)(2,1)}), bf16[16,8,4,4096]{3,2,1,0:T(4,128)(2,1)}, u32[]{:S(2)}, u32[]{:S(2)}) async-start(bf16[16,8,4,4096]{3,2,1,0:T(4,128)(2,1)} %stack.29), calls=%async_computation.3 | async-start | bytes 8388608 | tf_op jit(solution)/shard_map/all_to_all | solution.py:13
  355.9 7.6 %copy-start.1 = (bf16[2,64,4,4096]{3,2,1,0:T(4,128)(2,1)S(1)}, bf16[2,64,4,4096]{3,2,1,0:T(4,128)(2,1)}, u32[]{:S(2)}) copy-start(bf16[2,64,4,4096]{3,2,1,0:T(4,128)(2,1)} %all_to_all.91) | copy-start | bytes 12582916
  566.9 111.9 %copy-start.3 = (f32[3]{0:T(128)S(1)}, f32[3]{0:T(128)}, u32[]{:S(2)}) copy-start(f32[3]{0:T(128)} %param.5) | copy-start | bytes 40
